TPU v7x, 32 devices: a whole 2x2x4 slice. The times are simulated.
32 devices in a mesh: gx: 2 (over y), gy: 8 (over z, core), gz: 2 (over x).
Axes of the slice: x: 2, y: 2, z: 4, core: 2. Of those that a mesh axis runs over, the one named last changes fastest.
Arguments:
- starting_kelvin: float32 [16, 32, 2048], P(None, 'gx', ('gy', 'gz')), may hold values from -6 to 6
- substance_label: int32 [16, 32, 2048], P(None, 'gx', ('gy', 'gz')), may hold values from 0 to 3
- voxel_source_patch: int32 [16, 32, 2048], P(None, 'gx', ('gy', 'gz')), may hold values from 0 to 15
- substance_traits: float32 [4, 4], replicated, may hold values from 0.5 to 2
- patch_source_intensity: float32 [16], replicated, may hold values from 0 to 8
Outputs:
- warmed_result: float32 [16, 32, 2048], P(None, 'gx', ('gy', 'gz'))
- solution: float32 [3, 16, 32, 2048], P(None, 'gz', 'gx', 'gy')
- residual: float32 [3, 16, 32, 2048], P(None, 'gz', 'gx', 'gy')
All inputs are finite; a program needn't handle non-finite values.
Results may differ from a plain program's by a relative error of at most 0.0029.
Values sent between devices are 32-bit elements; how exact they have to be, the bound alone decides.
No kernel may reach another device: no remote copies, remote signals or barrier semaphores. Data moves between devices by JAX's collectives and lax.ppermute only.
A program may use at most 64 MiB of HBM per device.

v0:
```python
import functools

import jax
import jax.numpy as jnp
from jax import lax
from jax.experimental import pallas as pl
from jax.experimental.pallas import tpu as pltpu
from jax.sharding import PartitionSpec as P


ITERS = 3
HALO = 8
LANES = 128
PAD = 8
AXES = ("gx", "gy", "gz")

time_step = 0.03
anchor_scale = 0.5
strain_gain = 2.0
CENTRE = 55.0 / 9.0
K4 = 4.0 * (anchor_scale + CENTRE)

f32 = jnp.float32


def position():
    gx, gy, gz = (lax.axis_index(a) for a in AXES)
    ny, nz = lax.axis_size("gy"), lax.axis_size("gz")
    pos = gx ^ gz
    block = gy * nz + gz
    edge = jnp.where(pos == 0, 0, ny * nz - 1)
    return gx, gz, pos, block != edge


def lane_of(shape):
    return lax.broadcasted_iota(jnp.int32, shape, 1)


def pack_rows_kernel(
    traits, intensity, temp, label, patch, block, out, beside, across, table
):
    layers, rows, width = temp.shape
    groups = LANES // (2 * rows)
    deep = layers // groups
    pos = position()[2]
    kinds, count = traits.shape
    for k in range(kinds):
        for m in range(count):
            table[k * count + m] = jnp.full((8, LANES), traits[k, m], f32)
    for k in range(intensity.shape[0]):
        table[kinds * count + k] = jnp.full((8, LANES), intensity[k], f32)
    wide = width // 2 + HALO
    inner = pl.multiple_of((width - wide) * (1 - pos), 8)
    near = pl.multiple_of((width - HALO) * pos, 8)
    far = pl.multiple_of((width - HALO) * (1 - pos), 8)
    for a, ref in enumerate((temp, label, patch)):
        for p in range(deep // 2):
            parts = [ref[g * deep + 2 * p + j] for j in range(2) for g in range(groups)]
            block[a, p] = jnp.concatenate(parts, axis=0).astype(f32).T
            out[a, p] = block[a, p, pl.ds(inner, wide), :]
            beside[a, p] = block[a, p, pl.ds(near, HALO), :]
            across[a, p] = block[a, p, pl.ds(far, HALO), :]


def picks(ref, l, row):
    def at(dz, dx):
        return ref[l + 1 + dz, PAD + row + dx : PAD + row + dx + 8, :]

    out = {}
    for dx in (-1, 0, 1):
        up, mid, down = at(1, dx), at(0, dx), at(-1, dx)
        out["F", dx] = mid
        out["G", dx] = up + down
        out["H", dx] = up - down
    res = {}
    for k in "FGH":
        res[k] = out[k, 0]
        res["E" + k] = out[k, 1] + out[k, -1]
        res["D" + k] = out[k, 1] - out[k, -1]
    return res


def next_row(x, full):
    kept = lane_of(x.shape) % full != full - 1
    return jnp.where(kept, pltpu.roll(x, LANES - 1, 1), 0.0)


def last_row(x, full):
    kept = lane_of(x.shape) % full != 0
    return jnp.where(kept, pltpu.roll(x, 1, 1), 0.0)


def pair_sum(x, full):
    return next_row(x, full) + last_row(x, full)


def pair_difference(x, full):
    return next_row(x, full) - last_row(x, full)


def along_lanes(base, even, odd, full):
    return base + next_row(even + odd, full) + last_row(even - odd, full)


def wrap_layers(refs, full):
    for ref in refs:
        deep, height = ref.shape[-3] - 2, ref.shape[-2]
        for index in ([()] if len(ref.shape) == 3 else [(c,) for c in range(ref.shape[0])]):
            for r in range(PAD, height - PAD, 8):
                here = (slice(r, r + 8), slice(None))
                group = lane_of((8, LANES)) // full
                below = pltpu.roll(ref[index + (deep,) + here], full, 1)
                ref[index + (0,) + here] = jnp.where(group == 0, 0.0, below)
                above = pltpu.roll(ref[index + (1,) + here], LANES - full, 1)
                ref[index + (deep + 1,) + here] = jnp.where(
                    group == LANES // full - 1, 0.0, above
                )


N5 = 5.0 / 9.0
N2 = 2.0 / 9.0
N3 = 1.0 / 3.0


def full_stencil(z, x, y, full):
    base0 = z["EF"] + z["EG"] + 3.0 * z["G"] + 0.5 * x["DH"]
    even0 = z["F"] + z["G"] + 0.5 * z["EF"] + N5 * z["EG"] + N2 * x["DH"]
    odd0 = 0.5 * y["H"] + N2 * y["EH"]
    base1 = 3.0 * x["EF"] + x["G"] + x["EG"] + 0.5 * z["DH"]
    even1 = x["F"] + x["EF"] + 0.5 * x["G"] + N5 * x["EG"] + N2 * z["DH"]
    odd1 = 0.5 * y["DF"] + N2 * y["DG"]
    shared = y["EF"] + y["G"]
    base2 = shared + 0.5 * y["EG"]
    even2 = shared + 3.0 * y["F"] + N5 * y["EG"]
    odd2 = 0.5 * (x["DF"] + z["H"]) + N2 * (x["DG"] + z["EH"])
    return (
        along_lanes(base0, even0, odd0, full),
        along_lanes(base1, even1, odd1, full),
        along_lanes(base2, even2, odd2, full),
    )


def matrix_stencil(m, full):
    both = m["EF"] + m["EG"]
    shared = m["EF"] + m["G"]
    tail = N5 * m["EG"]
    zz = both + 3.0 * m["G"] + pair_sum(m["F"] + m["G"] + 0.5 * m["EF"] + tail, full)
    xx = 3.0 * m["EF"] + m["G"] + m["EG"] + pair_sum(m["F"] + m["EF"] + 0.5 * m["G"] + tail, full)
    yy = shared + 0.5 * m["EG"] + pair_sum(shared + 3.0 * m["F"] + tail, full)
    zx = 0.5 * m["DH"] + pair_sum(N2 * m["DH"], full)
    zy = pair_difference(0.5 * m["H"] + N2 * m["EH"], full)
    xy = pair_difference(0.5 * m["DF"] + N2 * m["DG"], full)
    return zz, xx, yy, zx, zy, xy


def gradient_stencil(f, full):
    gz = f["H"] + 0.5 * f["EH"] + pair_sum(0.5 * f["H"] + N3 * f["EH"], full)
    gx = f["DF"] + 0.5 * f["DG"] + pair_sum(0.5 * f["DF"] + N3 * f["DG"], full)
    gy = pair_difference(f["F"] + 0.5 * (f["G"] + f["EF"]) + N3 * f["EG"], full)
    return gz, gx, gy


def conduct(own, other):
    return 2.0 * own * other / jnp.maximum(own + other, 0.25)


def choose(label, values):
    out = jnp.zeros(label.shape, f32)
    for k, v in enumerate(values):
        out = jnp.where(label == float(k), v, out)
    return out


def shift_scale(table, count):
    total = table[2 * count]
    for k in range(1, count):
        total = total + table[2 * count + k]
    return total * ((anchor_scale + 2.0 * CENTRE) / count)


def packed_lanes(values, full, row_half, layer_half):
    lane = lane_of((8, LANES))
    rows = full // 2
    out = None
    for i, value in enumerate(values):
        target = (i // 2) * (LANES // 2) + (i % 2) * rows
        shift = target - layer_half * (LANES // 2) - row_half * rows + 2 * LANES
        moved = pltpu.roll(value, shift % LANES, 1)
        mine = ((lane // (LANES // 2)) == i // 2) & ((lane // rows) % 2 == i % 2)
        out = moved if out is None else jnp.where(mine, moved, out)
    return out


def pack_vectors(v, outs, warm, full):
    fields, deep, own, _ = v.shape
    gx, gz, _, _ = position()

    def piece(f, _):
        for number, out in enumerate(outs):
            row_half, layer_half = gx ^ (number % 2), gz ^ (number // 2)
            for r in range(0, own, 8):
                values = [v[f, i, r : r + 8, :] for i in range(deep)]
                out[f, r : r + 8, :] = packed_lanes(values, full, row_half, layer_half)
        return 0

    lax.fori_loop(0, fields, piece, 0)
    if warm is not None:
        for number in range(2):
            for layer_half in range(2):
                for r in range(0, own, 8):
                    values = [warm[i, r : r + 8, :] for i in range(deep)]
                    outs[number][fields + layer_half, r : r + 8, :] = packed_lanes(
                        values, full, gx ^ number, layer_half
                    )


def power_step(weight, mats, inside, source, dest, v, first_field, square_too, full):
    u, w = source
    deep, width = mats.shape[1], mats.shape[2]
    own = range(HALO, width - HALO, 8)
    tiles = own if dest is None else range(0, width, 8)

    def step(l, accs):
        accs = list(accs)
        for r in tiles:
            here = slice(PAD + r, PAD + r + 8)
            there = slice(r, r + 8)
            found, stencils = [], []
            for ref in (u, w):
                f = [picks(ref.at[c], l, r) for c in range(3)]
                found.append([x["F"] for x in f])
                stencils.append(full_stencil(*f, full))
            old, weighted = found
            cu, cw = stencils
            zz, xx, yy, zx, zy, xy = (mats[k, l, there, :] for k in range(6))
            mixed = (
                zz * old[0] + zx * old[1] + zy * old[2],
                zx * old[0] + xx * old[1] + xy * old[2],
                zy * old[0] + xy * old[1] + yy * old[2],
            )
            m = weight[l, there, :]
            keep = inside[there, :]
            for c in range(3):
                new = (K4 * weighted[c] + mixed[c] - m * cu[c] - cw[c]) * keep
                if dest is not None:
                    dest[0][c, l + 1, here, :] = new
                    dest[1][c, l + 1, here, :] = new * m
                if r in own:
                    v[first_field + c, l, r - HALO : r - HALO + 8, :] = new
                    accs[0] = accs[0] + new * old[c]
                    if square_too:
                        accs[1] = accs[1] + new * new
        return tuple(accs)

    zero = jnp.zeros((8, LANES), f32)
    accs = lax.fori_loop(0, deep, step, (zero,) * (2 if square_too else 1))
    if dest is not None:
        wrap_layers(dest, full)
    return accs


def clear_edges(refs):
    edge = jnp.zeros((PAD, LANES), f32)
    for ref in refs:
        height = ref.shape[-2]
        for index in ([()] if len(ref.shape) == 3 else [(c,) for c in range(ref.shape[0])]):
            for l in range(ref.shape[-3]):
                ref[index + (l, slice(0, PAD))] = edge
                ref[index + (l, slice(height - PAD, height))] = edge


def first_kernel(
    table, block, got, beside, across,
    weight, mats, inside, u_next, w_next, moments, mine, to_x, to_z, to_both,
    cond, temp_a, temp_b, cap, power, gz, gx, gy, gy_back, expand, strain, prod, u, w, v, warm,
    mod, source, win,
    *, count, full,
):
    pairs, wide = got.shape[1], got.shape[2]
    deep, width = mats.shape[1], mats.shape[2]
    rows = full // 2
    groups = LANES // full
    me, _, pos, paired = position()
    tiles = range(0, width, 8)
    kinds = 4
    sources = table.shape[0] - kinds * count

    inv_scale = 1.0 / shift_scale(table, count)
    cond_t = [table[k] for k in range(count)]
    cap_t = [time_step / table[count + k] for k in range(count)]
    mod_t = [table[2 * count + k] for k in range(count)]
    exp_t = [table[3 * count + k] for k in range(count)]
    pow_t = [table[kinds * count + k] for k in range(sources)]

    clear_edges((cond, temp_a, temp_b, mod, strain, prod, u, w, u_next, w_next))
    for l in range(deep):
        gx[l, 0:PAD] = jnp.zeros((PAD, LANES), f32)

    body = pl.multiple_of(HALO * (1 - pos), 8)
    strip = pl.multiple_of((width - HALO) * pos, 8)
    inner = pl.multiple_of((block.shape[2] - wide) * pos, 8)
    for a in range(3):
        for p in range(pairs):
            source[me, a * pairs + p, pl.ds(body, wide), :] = block[a, p, pl.ds(inner, wide), :]
            source[1 - me, a * pairs + p, pl.ds(body, wide), :] = got[a, p]
            for half, ref in ((me, beside), (1 - me, across)):
                value = ref[a, p]
                if a == 1:
                    value = jnp.where(paired, value, -1.0)
                source[half, a * pairs + p, pl.ds(strip, HALO), :] = value

    def window(k, _):
        lane = lane_of((8, LANES))
        for r in tiles:
            for j in range(2):
                value = None
                for half in range(2):
                    read = source[half, k, r : r + 8, :]
                    for g in range(groups):
                        shift = (g * full + half * rows - j * (LANES // 2) - g * rows) % LANES
                        moved = pltpu.roll(read, shift, 1) if shift else read
                        if value is None:
                            value = moved
                        else:
                            value = jnp.where(lane // rows == 2 * g + half, moved, value)
                win[2 * k + j, r : r + 8, :] = value
        return 0

    lax.fori_loop(0, 3 * pairs, window, 0)

    def looked_up(l, _):
        for r in tiles:
            here = slice(PAD + r, PAD + r + 8)
            there = slice(r, r + 8)
            temp_a[l + 1, here, :] = win[l, there, :]
            lab = win[deep + l, there, :]
            src = win[2 * deep + l, there, :]
            cond[l + 1, here, :] = choose(lab, cond_t)
            cap[l, there, :] = choose(lab, cap_t)
            mod[l + 1, here, :] = choose(lab, mod_t)
            expand[l, there, :] = choose(lab, exp_t)
            power[l, there, :] = choose(src, pow_t)
            inside[there, :] = jnp.where(lab >= 0.0, 1.0, 0.0)
        return 0

    lax.fori_loop(0, deep, looked_up, 0)
    wrap_layers((temp_a, cond, mod), full)

    for r in tiles:
        here = slice(PAD + r, PAD + r + 8)
        gz[0, r : r + 8, :] = conduct(cond[0, here, :], cond[1, here, :])

    def faces(l, _):
        for r in tiles:
            here = slice(PAD + r, PAD + r + 8)
            there = slice(r, r + 8)
            a = cond[l + 1, here, :]
            gz[l + 1, there, :] = conduct(a, cond[l + 2, here, :])
            gx[l, here, :] = conduct(a, cond[l + 1, PAD + r + 1 : PAD + r + 9, :])
            gy[l, there, :] = conduct(a, next_row(a, full))
            gy_back[l, there, :] = conduct(a, last_row(a, full))
        return 0

    lax.fori_loop(0, deep, faces, 0)

    def heat(src, dst, last):
        def step(l, _):
            for r in tiles:
                here = slice(PAD + r, PAD + r + 8)
                there = slice(r, r + 8)
                t = src[l + 1, here, :]
                flux = gz[l + 1, there, :] * (src[l + 2, here, :] - t)
                flux += gz[l, there, :] * (src[l, here, :] - t)
                flux += gx[l, here, :] * (src[l + 1, PAD + r + 1 : PAD + r + 9, :] - t)
                flux += gx[l, PAD + r - 1 : PAD + r + 7, :] * (
                    src[l + 1, PAD + r - 1 : PAD + r + 7, :] - t
                )
                flux += gy[l, there, :] * (pltpu.roll(t, LANES - 1, 1) - t)
                flux += gy_back[l, there, :] * (pltpu.roll(t, 1, 1) - t)
                new = t + cap[l, there, :] * (flux + power[l, there, :])
                if last:
                    if HALO <= r < width - HALO:
                        warm[l, r - HALO : r - HALO + 8, :] = new
                    s = expand[l, there, :] * new
                    strain[l + 1, here, :] = s
                    prod[l + 1, here, :] = s * mod[l + 1, here, :]
                else:
                    dst[l + 1, here, :] = new
            return 0

        lax.fori_loop(0, deep, step, 0, unroll=2)

    heat(temp_a, temp_b, False)
    wrap_layers((temp_b,), full)
    heat(temp_b, None, True)
    wrap_layers((strain, prod), full)

    quarter_scale = 0.25 * inv_scale

    def loads(l, acc):
        for r in tiles:
            here = slice(PAD + r, PAD + r + 8)
            there = slice(r, r + 8)
            s = picks(strain, l, r)
            m = picks(mod, l, r)
            q = picks(prod, l, r)
            gs, gm, gq = (gradient_stencil(f, full) for f in (s, m, q))
            for k, entry in enumerate(matrix_stencil(m, full)):
                entry = entry * quarter_scale
                mats[k, l, there, :] = entry - 1.0 if k < 3 else entry
            scaled = m["F"] * quarter_scale
            weight[l, there, :] = scaled
            keep = inside[there, :] * (-0.25 * strain_gain)
            for c in range(3):
                new = (m["F"] * gs[c] + s["F"] * gm[c] + gq[c]) * keep
                u[c, l + 1, here, :] = new
                w[c, l + 1, here, :] = new * scaled
                if HALO <= r < width - HALO:
                    v[c, l, r - HALO : r - HALO + 8, :] = new
                    acc = acc + new * new
        return acc

    moments[0] = lax.fori_loop(0, deep, loads, jnp.zeros((8, LANES), f32))
    wrap_layers((u, w), full)
    cross, square = power_step(
        weight, mats, inside, (u, w), (u_next, w_next), v, 3, True, full
    )
    moments[1] = cross
    moments[2] = square
    pack_vectors(v, (mine, to_x, to_z, to_both), warm, full)


def second_kernel(
    weight, mats, inside, u, w, moments,
    mom_out, mine, to_x, to_z, to_both,
    u_next, w_next, v,
    *, full,
):
    clear_edges((u_next, w_next))
    parts = [moments[k] for k in range(moments.shape[0])]
    parts += power_step(weight, mats, inside, (u, w), (u_next, w_next), v, 0, True, full)
    parts += power_step(weight, mats, inside, (u_next, w_next), None, v, 3, False, full)
    lane1 = lane_of((1, LANES))
    row = jnp.zeros((1, LANES), f32)
    for k, part in enumerate(parts):
        lanes = jnp.sum(part, axis=0, keepdims=True)
        row = jnp.where(lane1 == k, jnp.sum(lanes, axis=1, keepdims=True), row)
    for k in range(mom_out.shape[0]):
        mom_out[k] = row
    pack_vectors(v, (mine, to_x, to_z, to_both), None, full)


def coefficients(mu, scale):
    def inner(a, b):
        total = None
        for i, x in enumerate(a):
            for j, y in enumerate(b):
                term = x * y * mu[i + j]
                total = term if total is None else total + term
        return total

    def added(a, b):
        out = []
        for k in range(max(len(a), len(b))):
            if k >= len(a):
                out.append(b[k])
            elif k >= len(b):
                out.append(a[k])
            else:
                out.append(a[k] + b[k])
        return out

    one = jnp.ones_like(mu[0])
    residual = [one]
    direction = [one]
    solution = []
    norm = mu[0]
    for number in range(ITERS):
        image = added(direction, [jnp.zeros_like(one)] + direction)
        alpha = norm / inner(direction, image)
        solution = added(solution, [alpha * d for d in direction])
        residual = added(residual, [-alpha * d for d in image])
        if number + 1 < ITERS:
            following = inner(residual, residual)
            ratio = following / norm
            direction = added(residual, [ratio * d for d in direction])
            norm = following
    return [s / scale for s in solution], residual


def place_kernel(table, mom, *refs, count, full):
    early, late, outs, board = refs[:4], refs[4:8], refs[8:11], refs[11]
    warm_out, sol_out, res_out = outs
    layers, rows, _ = warm_out.shape
    deep = layers // (LANES // full)
    own = early[2].shape[1]
    _, gz, pos, _ = position()
    shape = (8, LANES)
    total = jnp.broadcast_to(jnp.sum(mom[:, 0, :], axis=0, keepdims=True), shape)
    mu = []
    for k in range(2 * ITERS):
        picked = jnp.where(lane_of(shape) == k, total, 0.0)
        mu.append(jnp.broadcast_to(jnp.sum(picked, axis=1, keepdims=True), shape))
    sol, res = coefficients(mu, shift_scale(table, count))

    def spread(slot, out, lanes, layer0):
        turned = board[slot].T
        for i in range(deep):
            for g in range(2):
                at = (i // 2) * (LANES // 2) + g * full + (i % 2) * rows
                out[layer0 + g * deep + i, :, lanes] = turned[at : at + rows]

    for half in range(2):
        for number in range(2):
            at = pl.multiple_of((pos ^ number) * own, own)
            board[half, pl.ds(at, own), :] = early[number][6 + half]
        spread(half, warm_out, slice(None), half * (layers // 2))
    slot = 2
    for block in range(2):
        lanes = pl.ds(pl.multiple_of((gz ^ block) * LANES, LANES), LANES)
        for c in range(3):
            for number in range(2):
                a, b = early[2 * block + number], late[2 * block + number]
                at = pl.multiple_of((pos ^ block ^ number) * own, own)
                for r in range(0, own, 8):
                    there = slice(r, r + 8)
                    values = (a[c, there, :], a[3 + c, there, :], b[c, there, :], b[3 + c, there, :])
                    x = sol[0] * values[0]
                    y = res[0] * values[0]
                    for k in range(1, ITERS + 1):
                        if k < ITERS:
                            x = x + sol[k] * values[k]
                        y = y + res[k] * values[k]
                    board[slot, pl.ds(at + r, 8), :] = x
                    board[slot + 1, pl.ds(at + r, 8), :] = y
            spread(slot, sol_out.at[(0, 2, 1)[c]], lanes, 0)
            spread(slot + 1, res_out.at[(0, 2, 1)[c]], lanes, 0)
            slot += 2


LIMIT = 28 * 1024 * 1024


def params():
    return pltpu.CompilerParams(vmem_limit_bytes=LIMIT)


def vmem():
    return pl.BlockSpec(memory_space=pltpu.VMEM)


def smem():
    return pl.BlockSpec(memory_space=pltpu.SMEM)


def per_device_fast(temp, label, patch, traits, intensity):
    nx, ny, nz = (lax.axis_size(a) for a in AXES)
    layers, rows, width = temp.shape
    full = rows * nx
    half = layers // 2
    devices = nx * ny * nz

    def number(x, b):
        return x * ny * nz + b

    def everywhere(dx, dz):
        return [
            (number(x, y * nz + z), number(x ^ dx, y * nz + (z ^ dz)))
            for x in range(nx) for y in range(ny) for z in range(nz)
        ]

    def side(x, b):
        return x ^ (b % nz)

    chain = []
    for b in range(1, ny * nz):
        left = [x for x in range(nx) if side(x, b - 1) == 1][0]
        right = [x for x in range(nx) if side(x, b) == 0][0]
        chain += [(number(left, b - 1), number(right, b)), (number(right, b), number(left, b - 1))]

    cross = []
    for x in range(nx):
        for b in range(ny * nz):
            toward = b - 1 if side(x, b) == 0 else b + 1
            if 0 <= toward < ny * nz:
                cross.append((number(x ^ 1, toward), number(x, b)))

    sds = lambda *s: jax.ShapeDtypeStruct(s, f32)
    held = lambda *s: pltpu.VMEM(s, f32)
    keep = lambda x: pltpu.with_memory_space_constraint(x, pltpu.VMEM)
    there = lambda x: pltpu.with_memory_space_constraint(x, pltpu.HBM)
    count = traits.shape[1]
    entries = traits.size + intensity.size
    groups = LANES // full
    deep = layers // groups
    mid = width // 2
    wide = mid + HALO
    own, to_partner, to_beside, to_across, table = pl.pallas_call(
        pack_rows_kernel,
        out_shape=(
            held(3, deep // 2, width, LANES), held(3, deep // 2, wide, LANES),
            held(3, deep // 2, HALO, LANES), held(3, deep // 2, HALO, LANES),
            held(entries, 8, LANES),
        ),
        in_specs=[smem(), smem(), vmem(), vmem(), vmem()],
        out_specs=(vmem(),) * 5,
        compiler_params=params(),
        name="pack_rows",
    )(there(traits), there(intensity), there(temp), there(label), there(patch))
    own, table = keep(own), keep(table)
    got = lax.ppermute(to_partner, AXES, everywhere(1, 0))
    across = lax.ppermute(to_across, AXES, cross)
    beside = lax.ppermute(to_beside, AXES, chain)
    got, across, beside = keep(got), keep(across), keep(beside)

    span = mid + 2 * HALO
    edged = (deep + 2, span + 2 * PAD, LANES)
    plain = (deep, span, LANES)
    padded = pltpu.VMEM(edged, f32)
    flat = pltpu.VMEM(plain, f32)
    vectors = pltpu.VMEM((3,) + edged, f32)
    packed = pltpu.VMEM((6, deep, mid, LANES), f32)
    first = pl.pallas_call(
        functools.partial(first_kernel, count=count, full=full),
        out_shape=(
            held(*plain), held(6, *plain), held(span, LANES), held(3, *edged), held(3, *edged),
            held(3, 8, LANES),
        ) + tuple(held(k, mid, LANES) for k in (8, 8, 6, 6)),
        in_specs=[vmem()] * 5,
        out_specs=(vmem(),) * 10,
        scratch_shapes=[
            padded, padded, padded, flat, flat,
            pltpu.VMEM((deep + 1, span, LANES), f32),
            pltpu.VMEM((deep, span + 2 * PAD, LANES), f32), flat, flat,
            flat, padded, padded, vectors, vectors,
            packed, pltpu.VMEM((deep, mid, LANES), f32), padded,
            pltpu.VMEM((2, 3 * (deep // 2), span, LANES), f32),
            pltpu.VMEM((3 * deep, span, LANES), f32),
        ],
        compiler_params=params(),
        name="first",
    )(table, own, got, beside, across)
    carried, early = first[:6], first[6:]

    def exchanged(mine, *pieces):
        moved = [mine]
        for (dx, dz), piece in zip(((1, 0), (0, 1), (1, 1)), pieces):
            moved.append(lax.ppermute(piece, AXES, everywhere(dx, dz)))
        return tuple(keep(x) for x in moved)

    early = exchanged(*early)
    second = pl.pallas_call(
        functools.partial(second_kernel, full=full),
        out_shape=(held(devices, 1, LANES),)
        + tuple(held(6, mid, LANES) for _ in range(4)),
        in_specs=[vmem()] * 6,
        out_specs=(vmem(),) * 5,
        scratch_shapes=[vectors, vectors, packed],
        compiler_params=params(),
        name="second",
    )(*(keep(x) for x in carried))
    late = exchanged(*second[1:])
    mom = lax.all_to_all(second[0], AXES, 0, 0, tiled=True)
    mom = keep(mom)
    return pl.pallas_call(
        functools.partial(place_kernel, count=count, full=full),
        out_shape=(
            sds(layers, rows, width),
            sds(3, half, rows, nz * width),
            sds(3, half, rows, nz * width),
        ),
        in_specs=[vmem()] * 10,
        out_specs=(vmem(),) * 3,
        scratch_shapes=[pltpu.VMEM((14, width, LANES), f32)],
        compiler_params=params(),
        name="place",
    )(table, mom, *early, *late)


def padded(value, sides, width):
    for axis, dim in sides:
        devices, length = (lax.axis_size(axis), value.shape[dim])
        up = [(i, (i + 1) % devices) for i in range(devices - 1)]
        down = [(j, i) for i, j in up]
        last = lax.slice_in_dim(value, length - width, length, axis=dim)
        initial = lax.slice_in_dim(value, 0, width, axis=dim)
        before = lax.ppermute(last, axis, up)
        after = lax.ppermute(initial, axis, down)
        value = jnp.concatenate([before, value, after], axis=dim)
    return value


def lookup(identity, table, count):
    summed = jnp.zeros(identity.shape, jnp.float32)
    for number in range(count):
        summed = summed + jnp.where(identity == number, table[number], jnp.float32(0.0))
    return summed


def heat_step(padded_temp, padded_cond, power, inverse_cap):
    centre = padded_temp[:, 1:-1, 1:-1]
    own = padded_cond[:, 1:-1, 1:-1]
    layers, rows, columns = centre.shape
    heat_flux = jnp.zeros_like(centre)
    for row_offset, column_offset in ((0, 1), (2, 1), (1, 0), (1, 2)):
        neighbour = padded_temp[
            :, row_offset : row_offset + rows, column_offset : column_offset + columns
        ]
        other = padded_cond[
            :, row_offset : row_offset + rows, column_offset : column_offset + columns
        ]
        heat_flux = heat_flux + conduct(own, other) * (neighbour - centre)
    vertical_temp = jnp.pad(centre, ((1, 1), (0, 0), (0, 0)))
    vertical_cond = jnp.pad(own, ((1, 1), (0, 0), (0, 0)))
    for layer_offset in (0, 2):
        other = vertical_cond[layer_offset : layer_offset + layers]
        neighbour = vertical_temp[layer_offset : layer_offset + layers]
        heat_flux = heat_flux + conduct(own, other) * (neighbour - centre)
    return centre + time_step * inverse_cap * (heat_flux + power)


def neighbour_offsets():
    listed = []
    for along_z in (-1, 0, 1):
        for along_x in (-1, 0, 1):
            for along_y in (-1, 0, 1):
                if along_z != 0 or along_x != 0 or along_y != 0:
                    listed.append((along_z, along_x, along_y))
    return listed


def apply_operator(field, padded_field, modulus, padded_modulus):
    layers, rows, columns = modulus.shape
    parts = [
        anchor_scale * modulus * field[0],
        anchor_scale * modulus * field[1],
        anchor_scale * modulus * field[2],
    ]
    for along_z, along_x, along_y in neighbour_offsets():
        length_sq = along_z * along_z + along_x * along_x + along_y * along_y
        window = (
            slice(1 + along_z, 1 + along_z + layers),
            slice(1 + along_x, 1 + along_x + rows),
            slice(1 + along_y, 1 + along_y + columns),
        )
        weight = 0.5 / length_sq * (modulus + padded_modulus[window])
        change = [field[index_c] - padded_field[index_c][window] for index_c in range(3)]
        projected = (along_z * change[0] + along_x * change[1] + along_y * change[2]) / length_sq
        for index_c, direction_part in enumerate((along_z, along_x, along_y)):
            parts[index_c] = parts[index_c] + weight * (
                0.5 * change[index_c] + direction_part * projected
            )
    return jnp.stack(parts)


def thermal_load(modulus, padded_modulus, strain, padded_strain):
    layers, rows, columns = modulus.shape
    parts = [jnp.zeros_like(modulus), jnp.zeros_like(modulus), jnp.zeros_like(modulus)]
    for along_z, along_x, along_y in neighbour_offsets():
        length_sq = along_z * along_z + along_x * along_x + along_y * along_y
        window = (
            slice(1 + along_z, 1 + along_z + layers),
            slice(1 + along_x, 1 + along_x + rows),
            slice(1 + along_y, 1 + along_y + columns),
        )
        weight = 0.5 / length_sq * (modulus + padded_modulus[window])
        pushing = weight * (0.5 * (strain + padded_strain[window]))
        for index_c, direction_part in enumerate((along_z, along_x, along_y)):
            if direction_part != 0:
                parts[index_c] = parts[index_c] - strain_gain * direction_part * pushing
    return jnp.stack(parts)


def two_products(residual, image):
    return lax.psum((jnp.sum(residual * residual), jnp.sum(residual * image)), ("gx", "gy", "gz"))


def per_device_plain(
    starting_kelvin, substance_label, voxel_source_patch, substance_traits, patch_source_intensity
):
    count = substance_traits.shape[1]
    diffusive_coefficient = lookup(substance_label, substance_traits[0], count)
    inverse_cap = 1.0 / lookup(substance_label, substance_traits[1], count)
    power = lookup(voxel_source_patch, patch_source_intensity, patch_source_intensity.shape[0])
    padded_array = padded(
        jnp.stack([starting_kelvin, diffusive_coefficient]), (("gx", 2), (("gy", "gz"), 3)), 1
    )
    padded_cond = padded_array[1]
    warmed_result = heat_step(padded_array[0], padded_cond, power, inverse_cap)
    number = 0
    extended = padded(warmed_result, (("gx", 1), (("gy", "gz"), 2)), 1)
    warmed_result = heat_step(extended, padded_cond, power, inverse_cap)
    modulus = lookup(substance_label, substance_traits[2], count)
    strain = lookup(substance_label, substance_traits[3], count) * warmed_result
    fields = jnp.stack([modulus, strain])
    vertical_cycle = ((0, 0), (1, 1), (0, 0), (0, 0))
    padded_fields = jnp.pad(padded(fields, (("gx", 2), (("gy", "gz"), 3)), 1), vertical_cycle)

    def extend(field):
        return jnp.pad(padded(field, (("gx", 2), (("gy", "gz"), 3)), 1), vertical_cycle)

    modulus = fields[0]
    padded_modulus = padded_fields[0]
    load = thermal_load(modulus, padded_modulus, fields[1], padded_fields[1])

    def operate(field):
        return apply_operator(field, extend(field), modulus, padded_modulus)

    solution = jnp.zeros_like(load)
    residual = load
    image = operate(residual)
    norm_now, product = two_products(residual, image)
    alpha = norm_now / product
    direction, along_image = (residual, image)
    for number in range(ITERS):
        solution = solution + alpha * direction
        residual = residual - alpha * along_image
        if number + 1 < ITERS:
            image = operate(residual)
            norm_next, product = two_products(residual, image)
            ratio = norm_next / norm_now
            alpha = norm_next / (product - ratio * norm_next / alpha)
            direction = residual + ratio * direction
            along_image = image + ratio * along_image
            norm_now = norm_next
    joined = lax.all_to_all(
        jnp.concatenate([solution, residual]), "gz", split_axis=1, concat_axis=3, tiled=True
    )
    solution = joined[:3]
    residual = joined[3:]
    return (warmed_result, solution, residual)


def solution(mesh):
    in_specs = (
        P(None, "gx", ("gy", "gz")),
        P(None, "gx", ("gy", "gz")),
        P(None, "gx", ("gy", "gz")),
        P(),
        P(),
    )
    out_specs = (P(None, "gx", ("gy", "gz")), P(None, "gz", "gx", "gy"), P(None, "gz", "gx", "gy"))

    def per_device(temp, label, patch, traits, intensity):
        layers, rows, width = temp.shape
        fits = (
            mesh.shape["gx"] == 2
            and mesh.shape["gz"] == 2
            and width == LANES
            and rows % 8 == 0
            and LANES == 4 * 2 * rows
            and layers == 4 * 4
        )
        run = per_device_fast if fits else per_device_plain
        return run(temp, label, patch, traits, intensity)

    return jax.shard_map(
        per_device, mesh=mesh, in_specs=in_specs, out_specs=out_specs, check_vma=False
    )
```

profile of v0, /device:TPU:0, one launch (start us, length us, event | category | flops | bytes accessed | tf_op | source)
XLA Modules:
  0.0 51.4 jit_solution(17076726227223894451)
XLA Ops:
  0.6 1.2 %pack_rows.1 = (f32[3,2,128,128]{3,2,1,0:T(8,128)S(1)}, f32[3,2,72,128]{3,2,1,0:T(8,128)S(1)}, f32[3,2,8,128]{3,2,1,0:T(8,128)S(1)}, f32[3,2,8,128]{3,2,1,0:T(8,128)S(1)}, f32[32,8,128]{2,1,0:T(8,128)S(1)}) custom-call(f32[4,4]{1,0:T(4,128)} %traits.1, f32[16]{0:T(128)} %intensity.1, f32[16,16,128]{2,1,0:T(8,128)} %temp.1, s32[16,16,128]{2,1,0:T(8,128)} %label.1, ...), custom_call_target="tpu_custom_call" | custom-call | tf_op jit(solution)/shard_map/pack_rows/pallas_call | solution.py:598
  1.9 3.1 %collective-permute-start = (f32[3,2,72,128]{3,2,1,0:T(8,128)S(1)}, f32[3,2,72,128]{3,2,1,0:T(8,128)S(1)}, u32[]{:S(2)}, u32[]{:S(2)}) collective-permute-start(f32[3,2,72,128]{3,2,1,0:T(8,128)S(1)} %get-tuple-element.25), channel_id=1, source_target_pairs={{0,16},{1,17},{2,18},{3,19},{4,20},{5,21},{6,22},{7,23},{8,24},{9,... | collective-permute-start | bytes 663560 | tf_op jit(solution)/shard_map/ppermute | solution.py:611
  4.9 0.7 %collective-permute-start.1 = (f32[3,2,8,128]{3,2,1,0:T(8,128)S(1)}, f32[3,2,8,128]{3,2,1,0:T(8,128)S(1)}, u32[]{:S(2)}, u32[]{:S(2)}) collective-permute-start(f32[3,2,8,128]{3,2,1,0:T(8,128)S(1)} %get-tuple-element.26), channel_id=1, source_target_pairs={{16,17},{17,16},{1,2},{2,1},{18,19},{19,18},{3,4},{4,3},{20,21},{2... | collective-permute-start | bytes 73736 | tf_op jit(solution)/shard_map/ppermute | solution.py:613
  5.6 4.6 %collective-permute-start.2 = (f32[3,2,8,128]{3,2,1,0:T(8,128)S(1)}, f32[3,2,8,128]{3,2,1,0:T(8,128)S(1)}, u32[]{:S(2)}, u32[]{:S(2)}) collective-permute-start(f32[3,2,8,128]{3,2,1,0:T(8,128)S(1)} %get-tuple-element.27), channel_id=1, source_target_pairs={{18,1},{17,2},{20,3},{19,4},{22,5},{21,6},{24,7},{23,8},{26,9},{25... | collective-permute-start | bytes 73736 | tf_op jit(solution)/shard_map/ppermute | solution.py:612
  10.2 0.0 collective-permute-done.1.beside
  10.2 1.5 %collective-permute-done.2.across = f32[3,2,8,128]{3,2,1,0:T(8,128)S(1)} collective-permute-done((f32[3,2,8,128]{3,2,1,0:T(8,128)S(1)}, f32[3,2,8,128]{3,2,1,0:T(8,128)S(1)}, u32[]{:S(2)}, u32[]{:S(2)}) %collective-permute-start.2) | collective-permute-done | bytes 24608 | tf_op jit(solution)/shard_map/ppermute | solution.py:612
  11.7 0.0 collective-permute-done.got
  11.7 8.1 %first.1 = (f32[4,80,128]{2,1,0:T(8,128)S(1)}, f32[6,4,80,128]{3,2,1,0:T(8,128)S(1)}, f32[80,128]{1,0:T(8,128)S(1)}, f32[3,6,96,128]{3,2,1,0:T(8,128)S(1)}, f32[...) custom-call(f32[32,8,128]{2,1,0:T(8,128)S(1)} %get-tuple-element.23., ...), custom_call_target="tpu_custom_call" | custom-call | tf_op jit(solution)/shard_map/first/pallas_call | solution.py:623
  19.8 4.7 %second.1 = (f32[32,1,128]{2,1,0:T(1,128)S(1)}, f32[6,64,128]{2,1,0:T(8,128)S(1)}, f32[6,64,128]{2,1,0:T(8,128)S(1)}, f32[6,64,128]{2,1,0:T(8,128)S(1)}, f32[6,64,128]{2,1,0:T(8,128)S(1)}) custom-call(f32[4,80,128]{2,1,0:T(8,128)S(1)} %get-tuple-element.28.weight, f32[6,4,80,128]{3,2,1,0:T(8,128)S(1)} %get-tuple-element.29.mats, ...), custom_call_target="tpu_custom_call" | custom-call | tf_op jit(solution)/shard_map/second/pallas_call | solution.py:652
  24.5 3.8 %collective-permute-start.6 = (f32[6,64,128]{2,1,0:T(8,128)S(1)}, f32[6,64,128]{2,1,0:T(8,128)S(1)}, u32[]{:S(2)}, u32[]{:S(2)}) collective-permute-start(f32[6,64,128]{2,1,0:T(8,128)S(1)} %get-tuple-element.40), channel_id=1, source_target_pairs={{0,16},{1,17},{2,18},{3,19},{4,20},{5,21},{6,22},{7,23},{8,24},{9,... | collective-permute-start | bytes 589832 | tf_op jit(solution)/shard_map/ppermute | solution.py:648
  28.3 0.1 collective-permute-start.3
  28.4 0.9 %collective-permute-start.7 = (f32[6,64,128]{2,1,0:T(8,128)S(1)}, f32[6,64,128]{2,1,0:T(8,128)S(1)}, u32[]{:S(2)}, u32[]{:S(2)}) collective-permute-start(f32[6,64,128]{2,1,0:T(8,128)S(1)} %get-tuple-element.41), channel_id=1, source_target_pairs={{0,1},{1,0},{2,3},{3,2},{4,5},{5,4},{6,7},{7,6},{8,9},{9,8},{10,11... | collective-permute-start | bytes 589832 | tf_op jit(solution)/shard_map/ppermute | solution.py:648
  29.3 2.5 %collective-permute-start.8 = (f32[6,64,128]{2,1,0:T(8,128)S(1)}, f32[6,64,128]{2,1,0:T(8,128)S(1)}, u32[]{:S(2)}, u32[]{:S(2)}) collective-permute-start(f32[6,64,128]{2,1,0:T(8,128)S(1)} %get-tuple-element.42), channel_id=1, source_target_pairs={{0,17},{1,16},{2,19},{3,18},{4,21},{5,20},{6,23},{7,22},{8,25},{9,... | collective-permute-start | bytes 589832 | tf_op jit(solution)/shard_map/ppermute | solution.py:648
  31.8 0.1 collective-permute-start.4
  31.9 2.1 %collective-permute-done.6.refs_5_ = f32[6,64,128]{2,1,0:T(8,128)S(1)} collective-permute-done((f32[6,64,128]{2,1,0:T(8,128)S(1)}, f32[6,64,128]{2,1,0:T(8,128)S(1)}, u32[]{:S(2)}, u32[]{:S(2)}) %collective-permute-start.6) | collective-permute-done | bytes 196640 | tf_op jit(solution)/shard_map/ppermute | solution.py:648
  34.0 0.9 %collective-permute-start.5 = (f32[6,64,128]{2,1,0:T(8,128)S(1)}, f32[6,64,128]{2,1,0:T(8,128)S(1)}, u32[]{:S(2)}, u32[]{:S(2)}) collective-permute-start(f32[6,64,128]{2,1,0:T(8,128)S(1)} %get-tuple-element.38), channel_id=1, source_target_pairs={{0,17},{1,16},{2,19},{3,18},{4,21},{5,20},{6,23},{7,22},{8,25},{9,... | collective-permute-start | bytes 589832 | tf_op jit(solution)/shard_map/ppermute | solution.py:648
  34.8 15.1 %all_to_all.5.mom = f32[32,1,128]{2,1,0:T(1,128)S(1)} all-to-all(f32[32,1,128]{2,1,0:T(1,128)S(1)} %get-tuple-element.34), channel_id=1, replica_groups=mesh['gx'=2,'gy'=8,'gz'=2] {'gx','gy','gz'}, dimensions={0} | all-to-all | bytes 32768 | tf_op jit(solution)/shard_map/all_to_all | solution.py:663
  50.0 0.0 collective-permute-done.7.refs_6_
  50.0 0.0 collective-permute-done.8.refs_7_
  50.0 0.0 collective-permute-done.4.refs_2_
  50.0 0.0 collective-permute-done.5.refs_3_
  50.0 0.0 collective-permute-done.3.refs_1_
  50.0 1.4 %place.1 = (f32[16,16,128]{2,1,0:T(8,128)}, f32[3,8,16,256]{3,2,1,0:T(8,128)}, f32[3,8,16,256]{3,2,1,0:T(8,128)}) custom-call(f32[32,8,128]{2,1,0:T(8,128)S(1)} %get-tuple-element.23.table, f32[32,1,128]{2,1,0:T(1,128)S(1)} %all_to_all.5.mom, f32[8,64,128]{2,1,0:T(8,128)S(1)} %get-tuple-element.35.refs_0_, f32[8,64,128]{2,1,0:T(8,128)S(1)} %collective-permute-done.3.refs_1_, ...), custom_call_target="tpu_custom_call" | custom-call | tf_op jit(solution)/shard_map/place/pallas_call | solution.py:665
Async XLA Ops:
  1.9 9.9 %collective-permute-start = (f32[3,2,72,128]{3,2,1,0:T(8,128)S(1)}, f32[3,2,72,128]{3,2,1,0:T(8,128)S(1)}, u32[]{:S(2)}, u32[]{:S(2)}) collective-permute-start(f32[3,2,72,128]{3,2,1,0:T(8,128)S(1)} %get-tuple-element.25), channel_id=1, source_target_pairs={{0,16},{1,17},{2,18},{3,19},{4,20},{5,21},{6,22},{7,23},{8,24},{9,... | collective-permute-start | bytes 663560 | tf_op jit(solution)/shard_map/ppermute | solution.py:611
  4.9 5.3 %collective-permute-start.1 = (f32[3,2,8,128]{3,2,1,0:T(8,128)S(1)}, f32[3,2,8,128]{3,2,1,0:T(8,128)S(1)}, u32[]{:S(2)}, u32[]{:S(2)}) collective-permute-start(f32[3,2,8,128]{3,2,1,0:T(8,128)S(1)} %get-tuple-element.26), channel_id=1, source_target_pairs={{16,17},{17,16},{1,2},{2,1},{18,19},{19,18},{3,4},{4,3},{20,21},{2... | collective-permute-start | bytes 73736 | tf_op jit(solution)/shard_map/ppermute | solution.py:613
  5.6 6.1 %collective-permute-start.2 = (f32[3,2,8,128]{3,2,1,0:T(8,128)S(1)}, f32[3,2,8,128]{3,2,1,0:T(8,128)S(1)}, u32[]{:S(2)}, u32[]{:S(2)}) collective-permute-start(f32[3,2,8,128]{3,2,1,0:T(8,128)S(1)} %get-tuple-element.27), channel_id=1, source_target_pairs={{18,1},{17,2},{20,3},{19,4},{22,5},{21,6},{24,7},{23,8},{26,9},{25... | collective-permute-start | bytes 73736 | tf_op jit(solution)/shard_map/ppermute | solution.py:612
  24.5 9.4 %collective-permute-start.6 = (f32[6,64,128]{2,1,0:T(8,128)S(1)}, f32[6,64,128]{2,1,0:T(8,128)S(1)}, u32[]{:S(2)}, u32[]{:S(2)}) collective-permute-start(f32[6,64,128]{2,1,0:T(8,128)S(1)} %get-tuple-element.40), channel_id=1, source_target_pairs={{0,16},{1,17},{2,18},{3,19},{4,20},{5,21},{6,22},{7,23},{8,24},{9,... | collective-permute-start | bytes 589832 | tf_op jit(solution)/shard_map/ppermute | solution.py:648
  28.3 21.7 %collective-permute-start.3 = (f32[8,64,128]{2,1,0:T(8,128)S(1)}, f32[8,64,128]{2,1,0:T(8,128)S(1)}, u32[]{:S(2)}, u32[]{:S(2)}) collective-permute-start(f32[8,64,128]{2,1,0:T(8,128)S(1)} %get-tuple-element.36), channel_id=1, source_target_pairs={{0,16},{1,17},{2,18},{3,19},{4,20},{5,21},{6,22},{7,23},{8,24},{9,... | collective-permute-start | bytes 786440 | tf_op jit(solution)/shard_map/ppermute | solution.py:648
  28.4 21.6 %collective-permute-start.7 = (f32[6,64,128]{2,1,0:T(8,128)S(1)}, f32[6,64,128]{2,1,0:T(8,128)S(1)}, u32[]{:S(2)}, u32[]{:S(2)}) collective-permute-start(f32[6,64,128]{2,1,0:T(8,128)S(1)} %get-tuple-element.41), channel_id=1, source_target_pairs={{0,1},{1,0},{2,3},{3,2},{4,5},{5,4},{6,7},{7,6},{8,9},{9,8},{10,11... | collective-permute-start | bytes 589832 | tf_op jit(solution)/shard_map/ppermute | solution.py:648
  29.3 20.7 %collective-permute-start.8 = (f32[6,64,128]{2,1,0:T(8,128)S(1)}, f32[6,64,128]{2,1,0:T(8,128)S(1)}, u32[]{:S(2)}, u32[]{:S(2)}) collective-permute-start(f32[6,64,128]{2,1,0:T(8,128)S(1)} %get-tuple-element.42), channel_id=1, source_target_pairs={{0,17},{1,16},{2,19},{3,18},{4,21},{5,20},{6,23},{7,22},{8,25},{9,... | collective-permute-start | bytes 589832 | tf_op jit(solution)/shard_map/ppermute | solution.py:648
  31.8 18.2 %collective-permute-start.4 = (f32[6,64,128]{2,1,0:T(8,128)S(1)}, f32[6,64,128]{2,1,0:T(8,128)S(1)}, u32[]{:S(2)}, u32[]{:S(2)}) collective-permute-start(f32[6,64,128]{2,1,0:T(8,128)S(1)} %get-tuple-element.37), channel_id=1, source_target_pairs={{0,1},{1,0},{2,3},{3,2},{4,5},{5,4},{6,7},{7,6},{8,9},{9,8},{10,11... | collective-permute-start | bytes 589832 | tf_op jit(solution)/shard_map/ppermute | solution.py:648
  34.0 16.0 %collective-permute-start.5 = (f32[6,64,128]{2,1,0:T(8,128)S(1)}, f32[6,64,128]{2,1,0:T(8,128)S(1)}, u32[]{:S(2)}, u32[]{:S(2)}) collective-permute-start(f32[6,64,128]{2,1,0:T(8,128)S(1)} %get-tuple-element.38), channel_id=1, source_target_pairs={{0,17},{1,16},{2,19},{3,18},{4,21},{5,20},{6,23},{7,22},{8,25},{9,... | collective-permute-start | bytes 589832 | tf_op jit(solution)/shard_map/ppermute | solution.py:648
where the time goes:
time: 51.6 us; the launch traced here: 51.4 us
  starting transfers between devices  16.5 us (32%)
  Pallas kernels  15.4 us (30%)
  blocking collectives  15.1 us (29%)
  waiting for transfers between devices  3.63 us (7%)
  between operations  0.7 us (1%)
    all_to_all x1, blocking collectives, per_device_fast(): mom = lax.all_to_all(second[0], AXES, 0, 0, tiled=True)  15.1 us
    ppermute x6, starting transfers between devices, exchanged(): moved.append(lax.ppermute(piece, AXES, everywhere(dx, dz)))  8.17 us
    pallas_call x1, Pallas kernels, per_device_fast(): pl.pallas_call(functools.partial(first_kernel, count=count, full=full), o...  8.11 us
    pallas_call x1, Pallas kernels, per_device_fast(): pl.pallas_call(functools.partial(second_kernel, full=full), out_shape=(he...  4.69 us
    ppermute x1, starting transfers between devices, per_device_fast(): across = lax.ppermute(to_across, AXES, cross)  4.64 us
    ppermute x1, starting transfers between devices, per_device_fast(): got = lax.ppermute(to_partner, AXES, everywhere(1, 0))  3.06 us
    ppermute x6, waiting for transfers between devices, exchanged(): moved.append(lax.ppermute(piece, AXES, everywhere(dx, dz)))  2.14 us
    ppermute x1, waiting for transfers between devices, per_device_fast(): across = lax.ppermute(to_across, AXES, cross)  1.49 us
  transfers between devices with their start and end apart: 9, of which 2 were waited for; matrix products, arithmetic and copies ran while one was open for 0% of the time, Pallas kernels for 0%

commit v1 on v0

--- a/solution.py
+++ b/solution.py
@@ -55,7 +55,7 @@
     far = pl.multiple_of((width - HALO) * (1 - pos), 8)
     for a, ref in enumerate((temp, label, patch)):
         for p in range(deep // 2):
-            parts = [ref[g * deep + 2 * p + j] for j in range(2) for g in range(groups)]
+            parts = [ref[g * deep + 2 * p + j] for g in range(groups) for j in range(2)]
             block[a, p] = jnp.concatenate(parts, axis=0).astype(f32).T
             out[a, p] = block[a, p, pl.ds(inner, wide), :]
             beside[a, p] = block[a, p, pl.ds(near, HALO), :]
@@ -178,40 +178,49 @@
     return total * ((anchor_scale + 2.0 * CENTRE) / count)
 
 
-def packed_lanes(values, full, row_half, layer_half):
-    lane = lane_of((8, LANES))
-    rows = full // 2
-    out = None
-    for i, value in enumerate(values):
-        target = (i // 2) * (LANES // 2) + (i % 2) * rows
-        shift = target - layer_half * (LANES // 2) - row_half * rows + 2 * LANES
-        moved = pltpu.roll(value, shift % LANES, 1)
-        mine = ((lane // (LANES // 2)) == i // 2) & ((lane // rows) % 2 == i % 2)
-        out = moved if out is None else jnp.where(mine, moved, out)
-    return out
+def exchanged_lanes(x, y, distance, swap):
+    low = (lane_of(x.shape) // distance) % 2 == 0
+    y_up = pltpu.roll(y, distance, 1)
+    x_down = pltpu.roll(x, LANES - distance, 1)
+    first = jnp.where(low, x, y_up)
+    second = jnp.where(low, x_down, y)
+    return jnp.where(swap, second, first), jnp.where(swap, first, second)
+
+
+def owner_lanes(values, rows, swap_rows, swap_layers):
+    wide = LANES // 2
+    a = exchanged_lanes(values[0], values[2], wide, swap_layers)
+    b = exchanged_lanes(values[1], values[3], wide, swap_layers)
+    return [exchanged_lanes(x, y, rows, swap_rows) for x, y in zip(a, b)]
 
 
 def pack_vectors(v, outs, warm, full):
     fields, deep, own, _ = v.shape
+    rows = full // 2
     gx, gz, _, _ = position()
+    shape = (8, LANES)
+    swap_rows = jnp.broadcast_to(gx, shape) == 1
+    swap_layers = jnp.broadcast_to(gz, shape) == 1
 
     def piece(f, _):
-        for number, out in enumerate(outs):
-            row_half, layer_half = gx ^ (number % 2), gz ^ (number // 2)
-            for r in range(0, own, 8):
-                values = [v[f, i, r : r + 8, :] for i in range(deep)]
-                out[f, r : r + 8, :] = packed_lanes(values, full, row_half, layer_half)
+        for r in range(0, own, 8):
+            made = owner_lanes(
+                [v[f, i, r : r + 8, :] for i in range(deep)], rows, swap_rows, swap_layers
+            )
+            for number, out in enumerate(outs):
+                out[f, r : r + 8, :] = made[number // 2][number % 2]
         return 0
 
-    lax.fori_loop(0, fields, piece, 0)
+    lax.fori_loop(0, fields, piece, 0, unroll=2)
     if warm is not None:
-        for number in range(2):
-            for layer_half in range(2):
-                for r in range(0, own, 8):
-                    values = [warm[i, r : r + 8, :] for i in range(deep)]
-                    outs[number][fields + layer_half, r : r + 8, :] = packed_lanes(
-                        values, full, gx ^ number, layer_half
-                    )
+        never = jnp.zeros(shape, jnp.bool_)
+        for r in range(0, own, 8):
+            made = owner_lanes(
+                [warm[i, r : r + 8, :] for i in range(deep)], rows, swap_rows, never
+            )
+            for number in range(2):
+                for layer_half in range(2):
+                    outs[number][fields + layer_half, r : r + 8, :] = made[layer_half][number]
 
 
 def power_step(weight, mats, inside, source, dest, v, first_field, square_too, full):
@@ -279,7 +288,6 @@
     pairs, wide = got.shape[1], got.shape[2]
     deep, width = mats.shape[1], mats.shape[2]
     rows = full // 2
-    groups = LANES // full
     me, _, pos, paired = position()
     tiles = range(0, width, 8)
     kinds = 4
@@ -310,23 +318,14 @@
                 source[half, a * pairs + p, pl.ds(strip, HALO), :] = value
 
     def window(k, _):
-        lane = lane_of((8, LANES))
+        low = (lane_of((8, LANES)) // rows) % 2 == 0
         for r in tiles:
-            for j in range(2):
-                value = None
-                for half in range(2):
-                    read = source[half, k, r : r + 8, :]
-                    for g in range(groups):
-                        shift = (g * full + half * rows - j * (LANES // 2) - g * rows) % LANES
-                        moved = pltpu.roll(read, shift, 1) if shift else read
-                        if value is None:
-                            value = moved
-                        else:
-                            value = jnp.where(lane // rows == 2 * g + half, moved, value)
-                win[2 * k + j, r : r + 8, :] = value
+            x, y = source[0, k, r : r + 8, :], source[1, k, r : r + 8, :]
+            win[2 * k, r : r + 8, :] = jnp.where(low, x, pltpu.roll(y, rows, 1))
+            win[2 * k + 1, r : r + 8, :] = jnp.where(low, pltpu.roll(x, LANES - rows, 1), y)
         return 0
 
-    lax.fori_loop(0, 3 * pairs, window, 0)
+    lax.fori_loop(0, 3 * pairs, window, 0, unroll=2)
 
     def looked_up(l, _):
         for r in tiles:

time: 51.6 us -> 49.6 us (0.961)
  Pallas kernels: 15.4 us -> 13.4 us
    pallas_call x1, Pallas kernels: 8.11 us -> 6.61 us  [per_device_fast(): pl.pallas_call(functools.partial(first_kernel, count=count, full=full), o...]
where the time goes in v1:
time: 49.6 us; the launch traced here: 49.4 us
  starting transfers between devices  16.5 us (33%)
  blocking collectives  15.1 us (30%)
  Pallas kernels  13.4 us (27%)
  waiting for transfers between devices  3.63 us (7%)
  between operations  0.7 us (1%)
    all_to_all x1, blocking collectives, per_device_fast(): mom = lax.all_to_all(second[0], AXES, 0, 0, tiled=True)  15.1 us
    ppermute x6, starting transfers between devices, exchanged(): moved.append(lax.ppermute(piece, AXES, everywhere(dx, dz)))  8.17 us
    pallas_call x1, Pallas kernels, per_device_fast(): pl.pallas_call(functools.partial(first_kernel, count=count, full=full), o...  6.61 us
    ppermute x1, starting transfers between devices, per_device_fast(): across = lax.ppermute(to_across, AXES, cross)  4.64 us
    pallas_call x1, Pallas kernels, per_device_fast(): pl.pallas_call(functools.partial(second_kernel, full=full), out_shape=(he...  4.23 us
    ppermute x1, starting transfers between devices, per_device_fast(): got = lax.ppermute(to_partner, AXES, everywhere(1, 0))  3.06 us
    ppermute x6, waiting for transfers between devices, exchanged(): moved.append(lax.ppermute(piece, AXES, everywhere(dx, dz)))  2.14 us
    ppermute x1, waiting for transfers between devices, per_device_fast(): across = lax.ppermute(to_across, AXES, cross)  1.49 us
  transfers between devices with their start and end apart: 9, of which 2 were waited for; matrix products, arithmetic and copies ran while one was open for 0% of the time, Pallas kernels for 0%

profile of v1, /device:TPU:0, one launch (start us, length us, event | category | flops | bytes accessed | tf_op | source)
XLA Modules:
  0.0 49.4 jit_solution(3078361369696201511)
XLA Ops:
  0.6 1.2 %pack_rows.1 = (f32[3,2,128,128]{3,2,1,0:T(8,128)S(1)}, f32[3,2,72,128]{3,2,1,0:T(8,128)S(1)}, f32[3,2,8,128]{3,2,1,0:T(8,128)S(1)}, f32[3,2,8,128]{3,2,1,0:T(8,128)S(1)}, f32[32,8,128]{2,1,0:T(8,128)S(1)}) custom-call(f32[4,4]{1,0:T(4,128)} %traits.1, f32[16]{0:T(128)} %intensity.1, f32[16,16,128]{2,1,0:T(8,128)} %temp.1, s32[16,16,128]{2,1,0:T(8,128)} %label.1, ...), custom_call_target="tpu_custom_call" | custom-call | tf_op jit(solution)/shard_map/pack_rows/pallas_call | solution.py:597
  1.9 3.1 %collective-permute-start = (f32[3,2,72,128]{3,2,1,0:T(8,128)S(1)}, f32[3,2,72,128]{3,2,1,0:T(8,128)S(1)}, u32[]{:S(2)}, u32[]{:S(2)}) collective-permute-start(f32[3,2,72,128]{3,2,1,0:T(8,128)S(1)} %get-tuple-element.25), channel_id=1, source_target_pairs={{0,16},{1,17},{2,18},{3,19},{4,20},{5,21},{6,22},{7,23},{8,24},{9,... | collective-permute-start | bytes 663560 | tf_op jit(solution)/shard_map/ppermute | solution.py:610
  4.9 0.7 %collective-permute-start.1 = (f32[3,2,8,128]{3,2,1,0:T(8,128)S(1)}, f32[3,2,8,128]{3,2,1,0:T(8,128)S(1)}, u32[]{:S(2)}, u32[]{:S(2)}) collective-permute-start(f32[3,2,8,128]{3,2,1,0:T(8,128)S(1)} %get-tuple-element.26), channel_id=1, source_target_pairs={{16,17},{17,16},{1,2},{2,1},{18,19},{19,18},{3,4},{4,3},{20,21},{2... | collective-permute-start | bytes 73736 | tf_op jit(solution)/shard_map/ppermute | solution.py:612
  5.6 4.6 %collective-permute-start.2 = (f32[3,2,8,128]{3,2,1,0:T(8,128)S(1)}, f32[3,2,8,128]{3,2,1,0:T(8,128)S(1)}, u32[]{:S(2)}, u32[]{:S(2)}) collective-permute-start(f32[3,2,8,128]{3,2,1,0:T(8,128)S(1)} %get-tuple-element.27), channel_id=1, source_target_pairs={{18,1},{17,2},{20,3},{19,4},{22,5},{21,6},{24,7},{23,8},{26,9},{25... | collective-permute-start | bytes 73736 | tf_op jit(solution)/shard_map/ppermute | solution.py:611
  10.2 0.0 collective-permute-done.1.beside
  10.2 1.5 %collective-permute-done.2.across = f32[3,2,8,128]{3,2,1,0:T(8,128)S(1)} collective-permute-done((f32[3,2,8,128]{3,2,1,0:T(8,128)S(1)}, f32[3,2,8,128]{3,2,1,0:T(8,128)S(1)}, u32[]{:S(2)}, u32[]{:S(2)}) %collective-permute-start.2) | collective-permute-done | bytes 24608 | tf_op jit(solution)/shard_map/ppermute | solution.py:611
  11.7 0.0 collective-permute-done.got
  11.7 6.6 %first.1 = (f32[4,80,128]{2,1,0:T(8,128)S(1)}, f32[6,4,80,128]{3,2,1,0:T(8,128)S(1)}, f32[80,128]{1,0:T(8,128)S(1)}, f32[3,6,96,128]{3,2,1,0:T(8,128)S(1)}, f32[...) custom-call(f32[32,8,128]{2,1,0:T(8,128)S(1)} %get-tuple-element.23., ...), custom_call_target="tpu_custom_call" | custom-call | tf_op jit(solution)/shard_map/first/pallas_call | solution.py:622
  18.4 4.2 %second.1 = (f32[32,1,128]{2,1,0:T(1,128)S(1)}, f32[6,64,128]{2,1,0:T(8,128)S(1)}, f32[6,64,128]{2,1,0:T(8,128)S(1)}, f32[6,64,128]{2,1,0:T(8,128)S(1)}, f32[6,64,128]{2,1,0:T(8,128)S(1)}) custom-call(f32[4,80,128]{2,1,0:T(8,128)S(1)} %get-tuple-element.28.weight, f32[6,4,80,128]{3,2,1,0:T(8,128)S(1)} %get-tuple-element.29.mats, ...), custom_call_target="tpu_custom_call" | custom-call | tf_op jit(solution)/shard_map/second/pallas_call | solution.py:651
  22.6 3.8 %collective-permute-start.6 = (f32[6,64,128]{2,1,0:T(8,128)S(1)}, f32[6,64,128]{2,1,0:T(8,128)S(1)}, u32[]{:S(2)}, u32[]{:S(2)}) collective-permute-start(f32[6,64,128]{2,1,0:T(8,128)S(1)} %get-tuple-element.40), channel_id=1, source_target_pairs={{0,16},{1,17},{2,18},{3,19},{4,20},{5,21},{6,22},{7,23},{8,24},{9,... | collective-permute-start | bytes 589832 | tf_op jit(solution)/shard_map/ppermute | solution.py:647
  26.4 0.1 collective-permute-start.3
  26.4 0.9 %collective-permute-start.7 = (f32[6,64,128]{2,1,0:T(8,128)S(1)}, f32[6,64,128]{2,1,0:T(8,128)S(1)}, u32[]{:S(2)}, u32[]{:S(2)}) collective-permute-start(f32[6,64,128]{2,1,0:T(8,128)S(1)} %get-tuple-element.41), channel_id=1, source_target_pairs={{0,1},{1,0},{2,3},{3,2},{4,5},{5,4},{6,7},{7,6},{8,9},{9,8},{10,11... | collective-permute-start | bytes 589832 | tf_op jit(solution)/shard_map/ppermute | solution.py:647
  27.3 2.5 %collective-permute-start.8 = (f32[6,64,128]{2,1,0:T(8,128)S(1)}, f32[6,64,128]{2,1,0:T(8,128)S(1)}, u32[]{:S(2)}, u32[]{:S(2)}) collective-permute-start(f32[6,64,128]{2,1,0:T(8,128)S(1)} %get-tuple-element.42), channel_id=1, source_target_pairs={{0,17},{1,16},{2,19},{3,18},{4,21},{5,20},{6,23},{7,22},{8,25},{9,... | collective-permute-start | bytes 589832 | tf_op jit(solution)/shard_map/ppermute | solution.py:647
  29.9 0.1 collective-permute-start.4
  29.9 2.1 %collective-permute-done.6.refs_5_ = f32[6,64,128]{2,1,0:T(8,128)S(1)} collective-permute-done((f32[6,64,128]{2,1,0:T(8,128)S(1)}, f32[6,64,128]{2,1,0:T(8,128)S(1)}, u32[]{:S(2)}, u32[]{:S(2)}) %collective-permute-start.6) | collective-permute-done | bytes 196640 | tf_op jit(solution)/shard_map/ppermute | solution.py:647
  32.0 0.9 %collective-permute-start.5 = (f32[6,64,128]{2,1,0:T(8,128)S(1)}, f32[6,64,128]{2,1,0:T(8,128)S(1)}, u32[]{:S(2)}, u32[]{:S(2)}) collective-permute-start(f32[6,64,128]{2,1,0:T(8,128)S(1)} %get-tuple-element.38), channel_id=1, source_target_pairs={{0,17},{1,16},{2,19},{3,18},{4,21},{5,20},{6,23},{7,22},{8,25},{9,... | collective-permute-start | bytes 589832 | tf_op jit(solution)/shard_map/ppermute | solution.py:647
  32.9 15.1 %all_to_all.5.mom = f32[32,1,128]{2,1,0:T(1,128)S(1)} all-to-all(f32[32,1,128]{2,1,0:T(1,128)S(1)} %get-tuple-element.34), channel_id=1, replica_groups=mesh['gx'=2,'gy'=8,'gz'=2] {'gx','gy','gz'}, dimensions={0} | all-to-all | bytes 32768 | tf_op jit(solution)/shard_map/all_to_all | solution.py:662
  48.0 0.0 collective-permute-done.7.refs_6_
  48.0 0.0 collective-permute-done.8.refs_7_
  48.0 0.0 collective-permute-done.4.refs_2_
  48.0 0.0 collective-permute-done.5.refs_3_
  48.1 0.0 collective-permute-done.3.refs_1_
  48.1 1.4 %place.1 = (f32[16,16,128]{2,1,0:T(8,128)}, f32[3,8,16,256]{3,2,1,0:T(8,128)}, f32[3,8,16,256]{3,2,1,0:T(8,128)}) custom-call(f32[32,8,128]{2,1,0:T(8,128)S(1)} %get-tuple-element.23.table, f32[32,1,128]{2,1,0:T(1,128)S(1)} %all_to_all.5.mom, f32[8,64,128]{2,1,0:T(8,128)S(1)} %get-tuple-element.35.refs_0_, f32[8,64,128]{2,1,0:T(8,128)S(1)} %collective-permute-done.3.refs_1_, ...), custom_call_target="tpu_custom_call" | custom-call | tf_op jit(solution)/shard_map/place/pallas_call | solution.py:664
Async XLA Ops:
  1.9 9.9 %collective-permute-start = (f32[3,2,72,128]{3,2,1,0:T(8,128)S(1)}, f32[3,2,72,128]{3,2,1,0:T(8,128)S(1)}, u32[]{:S(2)}, u32[]{:S(2)}) collective-permute-start(f32[3,2,72,128]{3,2,1,0:T(8,128)S(1)} %get-tuple-element.25), channel_id=1, source_target_pairs={{0,16},{1,17},{2,18},{3,19},{4,20},{5,21},{6,22},{7,23},{8,24},{9,... | collective-permute-start | bytes 663560 | tf_op jit(solution)/shard_map/ppermute | solution.py:610
  4.9 5.3 %collective-permute-start.1 = (f32[3,2,8,128]{3,2,1,0:T(8,128)S(1)}, f32[3,2,8,128]{3,2,1,0:T(8,128)S(1)}, u32[]{:S(2)}, u32[]{:S(2)}) collective-permute-start(f32[3,2,8,128]{3,2,1,0:T(8,128)S(1)} %get-tuple-element.26), channel_id=1, source_target_pairs={{16,17},{17,16},{1,2},{2,1},{18,19},{19,18},{3,4},{4,3},{20,21},{2... | collective-permute-start | bytes 73736 | tf_op jit(solution)/shard_map/ppermute | solution.py:612
  5.6 6.1 %collective-permute-start.2 = (f32[3,2,8,128]{3,2,1,0:T(8,128)S(1)}, f32[3,2,8,128]{3,2,1,0:T(8,128)S(1)}, u32[]{:S(2)}, u32[]{:S(2)}) collective-permute-start(f32[3,2,8,128]{3,2,1,0:T(8,128)S(1)} %get-tuple-element.27), channel_id=1, source_target_pairs={{18,1},{17,2},{20,3},{19,4},{22,5},{21,6},{24,7},{23,8},{26,9},{25... | collective-permute-start | bytes 73736 | tf_op jit(solution)/shard_map/ppermute | solution.py:611
  22.6 9.4 %collective-permute-start.6 = (f32[6,64,128]{2,1,0:T(8,128)S(1)}, f32[6,64,128]{2,1,0:T(8,128)S(1)}, u32[]{:S(2)}, u32[]{:S(2)}) collective-permute-start(f32[6,64,128]{2,1,0:T(8,128)S(1)} %get-tuple-element.40), channel_id=1, source_target_pairs={{0,16},{1,17},{2,18},{3,19},{4,20},{5,21},{6,22},{7,23},{8,24},{9,... | collective-permute-start | bytes 589832 | tf_op jit(solution)/shard_map/ppermute | solution.py:647
  26.4 21.7 %collective-permute-start.3 = (f32[8,64,128]{2,1,0:T(8,128)S(1)}, f32[8,64,128]{2,1,0:T(8,128)S(1)}, u32[]{:S(2)}, u32[]{:S(2)}) collective-permute-start(f32[8,64,128]{2,1,0:T(8,128)S(1)} %get-tuple-element.36), channel_id=1, source_target_pairs={{0,16},{1,17},{2,18},{3,19},{4,20},{5,21},{6,22},{7,23},{8,24},{9,... | collective-permute-start | bytes 786440 | tf_op jit(solution)/shard_map/ppermute | solution.py:647
  26.4 21.6 %collective-permute-start.7 = (f32[6,64,128]{2,1,0:T(8,128)S(1)}, f32[6,64,128]{2,1,0:T(8,128)S(1)}, u32[]{:S(2)}, u32[]{:S(2)}) collective-permute-start(f32[6,64,128]{2,1,0:T(8,128)S(1)} %get-tuple-element.41), channel_id=1, source_target_pairs={{0,1},{1,0},{2,3},{3,2},{4,5},{5,4},{6,7},{7,6},{8,9},{9,8},{10,11... | collective-permute-start | bytes 589832 | tf_op jit(solution)/shard_map/ppermute | solution.py:647
  27.3 20.7 %collective-permute-start.8 = (f32[6,64,128]{2,1,0:T(8,128)S(1)}, f32[6,64,128]{2,1,0:T(8,128)S(1)}, u32[]{:S(2)}, u32[]{:S(2)}) collective-permute-start(f32[6,64,128]{2,1,0:T(8,128)S(1)} %get-tuple-element.42), channel_id=1, source_target_pairs={{0,17},{1,16},{2,19},{3,18},{4,21},{5,20},{6,23},{7,22},{8,25},{9,... | collective-permute-start | bytes 589832 | tf_op jit(solution)/shard_map/ppermute | solution.py:647
  29.9 18.2 %collective-permute-start.4 = (f32[6,64,128]{2,1,0:T(8,128)S(1)}, f32[6,64,128]{2,1,0:T(8,128)S(1)}, u32[]{:S(2)}, u32[]{:S(2)}) collective-permute-start(f32[6,64,128]{2,1,0:T(8,128)S(1)} %get-tuple-element.37), channel_id=1, source_target_pairs={{0,1},{1,0},{2,3},{3,2},{4,5},{5,4},{6,7},{7,6},{8,9},{9,8},{10,11... | collective-permute-start | bytes 589832 | tf_op jit(solution)/shard_map/ppermute | solution.py:647
  32.0 16.0 %collective-permute-start.5 = (f32[6,64,128]{2,1,0:T(8,128)S(1)}, f32[6,64,128]{2,1,0:T(8,128)S(1)}, u32[]{:S(2)}, u32[]{:S(2)}) collective-permute-start(f32[6,64,128]{2,1,0:T(8,128)S(1)} %get-tuple-element.38), channel_id=1, source_target_pairs={{0,17},{1,16},{2,19},{3,18},{4,21},{5,20},{6,23},{7,22},{8,25},{9,... | collective-permute-start | bytes 589832 | tf_op jit(solution)/shard_map/ppermute | solution.py:647

commit v2 on v1

--- a/solution.py
+++ b/solution.py
@@ -279,7 +279,7 @@
 
 
 def first_kernel(
-    table, block, got, beside, across,
+    table, block, got, beside,
     weight, mats, inside, u_next, w_next, moments, mine, to_x, to_z, to_both,
     cond, temp_a, temp_b, cap, power, gz, gx, gy, gy_back, expand, strain, prod, u, w, v, warm,
     mod, source, win,
@@ -311,8 +311,8 @@
         for p in range(pairs):
             source[me, a * pairs + p, pl.ds(body, wide), :] = block[a, p, pl.ds(inner, wide), :]
             source[1 - me, a * pairs + p, pl.ds(body, wide), :] = got[a, p]
-            for half, ref in ((me, beside), (1 - me, across)):
-                value = ref[a, p]
+            for k, half in enumerate((me, 1 - me)):
+                value = beside[k, a, p]
                 if a == 1:
                     value = jnp.where(paired, value, -1.0)
                 source[half, a * pairs + p, pl.ds(strip, HALO), :] = value
@@ -577,13 +577,6 @@
         right = [x for x in range(nx) if side(x, b) == 0][0]
         chain += [(number(left, b - 1), number(right, b)), (number(right, b), number(left, b - 1))]
 
-    cross = []
-    for x in range(nx):
-        for b in range(ny * nz):
-            toward = b - 1 if side(x, b) == 0 else b + 1
-            if 0 <= toward < ny * nz:
-                cross.append((number(x ^ 1, toward), number(x, b)))
-
     sds = lambda *s: jax.ShapeDtypeStruct(s, f32)
     held = lambda *s: pltpu.VMEM(s, f32)
     keep = lambda x: pltpu.with_memory_space_constraint(x, pltpu.VMEM)
@@ -607,10 +600,10 @@
         name="pack_rows",
     )(there(traits), there(intensity), there(temp), there(label), there(patch))
     own, table = keep(own), keep(table)
+    strip = lax.ppermute(to_across, AXES, everywhere(1, 0))
     got = lax.ppermute(to_partner, AXES, everywhere(1, 0))
-    across = lax.ppermute(to_across, AXES, cross)
-    beside = lax.ppermute(to_beside, AXES, chain)
-    got, across, beside = keep(got), keep(across), keep(beside)
+    beside = lax.ppermute(jnp.stack([to_beside, strip]), AXES, chain)
+    got, beside = keep(got), keep(beside)
 
     span = mid + 2 * HALO
     edged = (deep + 2, span + 2 * PAD, LANES)
@@ -625,7 +618,7 @@
             held(*plain), held(6, *plain), held(span, LANES), held(3, *edged), held(3, *edged),
             held(3, 8, LANES),
         ) + tuple(held(k, mid, LANES) for k in (8, 8, 6, 6)),
-        in_specs=[vmem()] * 5,
+        in_specs=[vmem()] * 4,
         out_specs=(vmem(),) * 10,
         scratch_shapes=[
             padded, padded, padded, flat, flat,
@@ -638,7 +631,7 @@
         ],
         compiler_params=params(),
         name="first",
-    )(table, own, got, beside, across)
+    )(table, own, got, beside)
     carried, early = first[:6], first[6:]
 
     def exchanged(mine, *pieces):

time: 49.6 us -> 53.1 us (1.071)
  waiting for transfers between devices: 3.63 us -> 8.77 us
  blocking collectives: 15.1 us -> 11.3 us
  starting transfers between devices: 16.5 us -> 18.7 us
    ppermute x6, starting transfers between devices: 8.17 us -> 15 us  [exchanged(): moved.append(lax.ppermute(piece, AXES, everywhere(dx, dz)))]
    ppermute x2, starting transfers between devices: 5.29 us -> 0.73 us  [the longest x1 0.65 us: per_device_fast(): beside = lax.ppermute(jnp.stack([to_beside, strip]), AXES, chain)]
    ppermute x2, waiting for transfers between devices: 1.49 us -> 5.88 us  [the longest x1 5.88 us: per_device_fast(): strip = lax.ppermute(to_across, AXES, everywhere(1, 0))]
    all_to_all x1, blocking collectives: 15.1 us -> 11.3 us  [per_device_fast(): mom = lax.all_to_all(second[0], AXES, 0, 0, tiled=True)]
    ppermute x6, waiting for transfers between devices: 2.14 us -> 2.89 us  [exchanged(): moved.append(lax.ppermute(piece, AXES, everywhere(dx, dz)))]
where the time goes in v2:
time: 53.1 us; the launch traced here: 53 us
  starting transfers between devices  18.7 us (35%)
  Pallas kernels  13.4 us (25%)
  blocking collectives  11.3 us (21%)
  waiting for transfers between devices  8.77 us (17%)
  between operations  0.7 us (1%)
    ppermute x6, starting transfers between devices, exchanged(): moved.append(lax.ppermute(piece, AXES, everywhere(dx, dz)))  15 us
    all_to_all x1, blocking collectives, per_device_fast(): mom = lax.all_to_all(second[0], AXES, 0, 0, tiled=True)  11.3 us
    pallas_call x1, Pallas kernels, per_device_fast(): pl.pallas_call(functools.partial(first_kernel, count=count, full=full), o...  6.61 us
    ppermute x1, waiting for transfers between devices, per_device_fast(): strip = lax.ppermute(to_across, AXES, everywhere(1, 0))  5.88 us
    pallas_call x1, Pallas kernels, per_device_fast(): pl.pallas_call(functools.partial(second_kernel, full=full), out_shape=(he...  4.23 us
    ppermute x1, starting transfers between devices, per_device_fast(): got = lax.ppermute(to_partner, AXES, everywhere(1, 0))  3.06 us
    ppermute x6, waiting for transfers between devices, exchanged(): moved.append(lax.ppermute(piece, AXES, everywhere(dx, dz)))  2.89 us
    pallas_call x1, Pallas kernels, per_device_fast(): pl.pallas_call(functools.partial(place_kernel, count=count, full=full), o...  1.37 us
  transfers between devices with their start and end apart: 9, of which 2 were waited for; matrix products, arithmetic and copies ran while one was open for 0% of the time, Pallas kernels for 0%

profile of v2, /device:TPU:0, one launch (start us, length us, event | category | flops | bytes accessed | tf_op | source)
XLA Modules:
  0.0 53.0 jit_solution(3020316548384296766)
XLA Ops:
  0.6 1.2 %pack_rows.1 = (f32[3,2,128,128]{3,2,1,0:T(8,128)S(1)}, f32[3,2,72,128]{3,2,1,0:T(8,128)S(1)}, f32[3,2,8,128]{3,2,1,0:T(8,128)S(1)}, f32[3,2,8,128]{3,2,1,0:T(8,128)S(1)}, f32[32,8,128]{2,1,0:T(8,128)S(1)}) custom-call(f32[4,4]{1,0:T(4,128)} %traits.1, f32[16]{0:T(128)} %intensity.1, f32[16,16,128]{2,1,0:T(8,128)} %temp.1, s32[16,16,128]{2,1,0:T(8,128)} %label.1, ...), custom_call_target="tpu_custom_call" | custom-call | tf_op jit(solution)/shard_map/pack_rows/pallas_call | solution.py:590
  1.9 3.1 %collective-permute-start = (f32[3,2,72,128]{3,2,1,0:T(8,128)S(1)}, f32[3,2,72,128]{3,2,1,0:T(8,128)S(1)}, u32[]{:S(2)}, u32[]{:S(2)}) collective-permute-start(f32[3,2,72,128]{3,2,1,0:T(8,128)S(1)} %get-tuple-element.25), channel_id=1, source_target_pairs={{0,16},{1,17},{2,18},{3,19},{4,20},{5,21},{6,22},{7,23},{8,24},{9,... | collective-permute-start | bytes 663560 | tf_op jit(solution)/shard_map/ppermute | solution.py:604
  4.9 0.1 collective-permute-start.1
  5.0 5.9 %collective-permute-done.1 = f32[3,2,8,128]{3,2,1,0:T(8,128)S(1)} collective-permute-done((f32[3,2,8,128]{3,2,1,0:T(8,128)S(1)}, f32[3,2,8,128]{3,2,1,0:T(8,128)S(1)}, u32[]{:S(2)}, u32[]{:S(2)}) %collective-permute-start.1) | collective-permute-done | bytes 24608 | tf_op jit(solution)/shard_map/ppermute | solution.py:603
  10.9 0.7 %collective-permute-start.2 = (f32[2,3,2,8,128]{4,3,2,1,0:T(8,128)S(1)}, f32[2,3,2,8,128]{4,3,2,1,0:T(8,128)S(1)}, u32[]{:S(2)}, u32[]{:S(2)}) collective-permute-start(f32[2,3,2,8,128]{4,3,2,1,0:T(8,128)S(1)} %pad_maximum_fusion), channel_id=1, source_target_pairs={{16,17},{17,16},{1,2},{2,1},{18,19},{19,18},{3,4},{4,3},{20,21},{2... | collective-permute-start | bytes 147464 | tf_op jit(solution)/shard_map/ppermute | solution.py:605
  11.5 0.0 collective-permute-done.2.beside
  11.6 0.0 collective-permute-done.got
  11.6 6.6 %first.1 = (f32[4,80,128]{2,1,0:T(8,128)S(1)}, f32[6,4,80,128]{3,2,1,0:T(8,128)S(1)}, f32[80,128]{1,0:T(8,128)S(1)}, f32[3,6,96,128]{3,2,1,0:T(8,128)S(1)}, f32[...) custom-call(f32[32,8,128]{2,1,0:T(8,128)S(1)} %get-tuple-element.23., ...), custom_call_target="tpu_custom_call" | custom-call | tf_op jit(solution)/shard_map/first/pallas_call | solution.py:615
  18.2 4.2 %second.1 = (f32[32,1,128]{2,1,0:T(1,128)S(1)}, f32[6,64,128]{2,1,0:T(8,128)S(1)}, f32[6,64,128]{2,1,0:T(8,128)S(1)}, f32[6,64,128]{2,1,0:T(8,128)S(1)}, f32[6,64,128]{2,1,0:T(8,128)S(1)}) custom-call(f32[4,80,128]{2,1,0:T(8,128)S(1)} %get-tuple-element.28.weight, f32[6,4,80,128]{3,2,1,0:T(8,128)S(1)} %get-tuple-element.29.mats, ...), custom_call_target="tpu_custom_call" | custom-call | tf_op jit(solution)/shard_map/second/pallas_call | solution.py:644
  22.4 7.1 %collective-permute-start.6 = (f32[6,64,128]{2,1,0:T(8,128)S(1)}, f32[6,64,128]{2,1,0:T(8,128)S(1)}, u32[]{:S(2)}, u32[]{:S(2)}) collective-permute-start(f32[6,64,128]{2,1,0:T(8,128)S(1)} %get-tuple-element.40), channel_id=1, source_target_pairs={{0,16},{1,17},{2,18},{3,19},{4,20},{5,21},{6,22},{7,23},{8,24},{9,... | collective-permute-start | bytes 589832 | tf_op jit(solution)/shard_map/ppermute | solution.py:640
  29.5 0.1 collective-permute-start.3
  29.6 1.9 %collective-permute-start.7 = (f32[6,64,128]{2,1,0:T(8,128)S(1)}, f32[6,64,128]{2,1,0:T(8,128)S(1)}, u32[]{:S(2)}, u32[]{:S(2)}) collective-permute-start(f32[6,64,128]{2,1,0:T(8,128)S(1)} %get-tuple-element.41), channel_id=1, source_target_pairs={{0,1},{1,0},{2,3},{3,2},{4,5},{5,4},{6,7},{7,6},{8,9},{9,8},{10,11... | collective-permute-start | bytes 589832 | tf_op jit(solution)/shard_map/ppermute | solution.py:640
  31.5 1.5 %collective-permute-start.8 = (f32[6,64,128]{2,1,0:T(8,128)S(1)}, f32[6,64,128]{2,1,0:T(8,128)S(1)}, u32[]{:S(2)}, u32[]{:S(2)}) collective-permute-start(f32[6,64,128]{2,1,0:T(8,128)S(1)} %get-tuple-element.42), channel_id=1, source_target_pairs={{0,17},{1,16},{2,19},{3,18},{4,21},{5,20},{6,23},{7,22},{8,25},{9,... | collective-permute-start | bytes 589832 | tf_op jit(solution)/shard_map/ppermute | solution.py:640
  33.0 1.5 %collective-permute-start.4 = (f32[6,64,128]{2,1,0:T(8,128)S(1)}, f32[6,64,128]{2,1,0:T(8,128)S(1)}, u32[]{:S(2)}, u32[]{:S(2)}) collective-permute-start(f32[6,64,128]{2,1,0:T(8,128)S(1)} %get-tuple-element.37), channel_id=1, source_target_pairs={{0,1},{1,0},{2,3},{3,2},{4,5},{5,4},{6,7},{7,6},{8,9},{9,8},{10,11... | collective-permute-start | bytes 589832 | tf_op jit(solution)/shard_map/ppermute | solution.py:640
  34.5 2.9 %collective-permute-done.6.refs_5_ = f32[6,64,128]{2,1,0:T(8,128)S(1)} collective-permute-done((f32[6,64,128]{2,1,0:T(8,128)S(1)}, f32[6,64,128]{2,1,0:T(8,128)S(1)}, u32[]{:S(2)}, u32[]{:S(2)}) %collective-permute-start.6) | collective-permute-done | bytes 196640 | tf_op jit(solution)/shard_map/ppermute | solution.py:640
  37.4 2.9 %collective-permute-start.5 = (f32[6,64,128]{2,1,0:T(8,128)S(1)}, f32[6,64,128]{2,1,0:T(8,128)S(1)}, u32[]{:S(2)}, u32[]{:S(2)}) collective-permute-start(f32[6,64,128]{2,1,0:T(8,128)S(1)} %get-tuple-element.38), channel_id=1, source_target_pairs={{0,17},{1,16},{2,19},{3,18},{4,21},{5,20},{6,23},{7,22},{8,25},{9,... | collective-permute-start | bytes 589832 | tf_op jit(solution)/shard_map/ppermute | solution.py:640
  40.3 11.3 %all_to_all.5.mom = f32[32,1,128]{2,1,0:T(1,128)S(1)} all-to-all(f32[32,1,128]{2,1,0:T(1,128)S(1)} %get-tuple-element.34), channel_id=1, replica_groups=mesh['gx'=2,'gy'=8,'gz'=2] {'gx','gy','gz'}, dimensions={0} | all-to-all | bytes 32768 | tf_op jit(solution)/shard_map/all_to_all | solution.py:655
  51.6 0.0 collective-permute-done.7.refs_6_
  51.6 0.0 collective-permute-done.8.refs_7_
  51.6 0.0 collective-permute-done.4.refs_2_
  51.6 0.0 collective-permute-done.5.refs_3_
  51.6 0.0 collective-permute-done.3.refs_1_
  51.6 1.4 %place.1 = (f32[16,16,128]{2,1,0:T(8,128)}, f32[3,8,16,256]{3,2,1,0:T(8,128)}, f32[3,8,16,256]{3,2,1,0:T(8,128)}) custom-call(f32[32,8,128]{2,1,0:T(8,128)S(1)} %get-tuple-element.23.table, f32[32,1,128]{2,1,0:T(1,128)S(1)} %all_to_all.5.mom, f32[8,64,128]{2,1,0:T(8,128)S(1)} %get-tuple-element.35.refs_0_, f32[8,64,128]{2,1,0:T(8,128)S(1)} %collective-permute-done.3.refs_1_, ...), custom_call_target="tpu_custom_call" | custom-call | tf_op jit(solution)/shard_map/place/pallas_call | solution.py:657
  (1 shorter events, 0.0 us)
Async XLA Ops:
  1.9 9.7 %collective-permute-start = (f32[3,2,72,128]{3,2,1,0:T(8,128)S(1)}, f32[3,2,72,128]{3,2,1,0:T(8,128)S(1)}, u32[]{:S(2)}, u32[]{:S(2)}) collective-permute-start(f32[3,2,72,128]{3,2,1,0:T(8,128)S(1)} %get-tuple-element.25), channel_id=1, source_target_pairs={{0,16},{1,17},{2,18},{3,19},{4,20},{5,21},{6,22},{7,23},{8,24},{9,... | collective-permute-start | bytes 663560 | tf_op jit(solution)/shard_map/ppermute | solution.py:604
  4.9 6.0 %collective-permute-start.1 = (f32[3,2,8,128]{3,2,1,0:T(8,128)S(1)}, f32[3,2,8,128]{3,2,1,0:T(8,128)S(1)}, u32[]{:S(2)}, u32[]{:S(2)}) collective-permute-start(f32[3,2,8,128]{3,2,1,0:T(8,128)S(1)} %get-tuple-element.27), channel_id=1, source_target_pairs={{0,16},{1,17},{2,18},{3,19},{4,20},{5,21},{6,22},{7,23},{8,24},{9,... | collective-permute-start | bytes 73736 | tf_op jit(solution)/shard_map/ppermute | solution.py:603
  10.9 0.7 %collective-permute-start.2 = (f32[2,3,2,8,128]{4,3,2,1,0:T(8,128)S(1)}, f32[2,3,2,8,128]{4,3,2,1,0:T(8,128)S(1)}, u32[]{:S(2)}, u32[]{:S(2)}) collective-permute-start(f32[2,3,2,8,128]{4,3,2,1,0:T(8,128)S(1)} %pad_maximum_fusion), channel_id=1, source_target_pairs={{16,17},{17,16},{1,2},{2,1},{18,19},{19,18},{3,4},{4,3},{20,21},{2... | collective-permute-start | bytes 147464 | tf_op jit(solution)/shard_map/ppermute | solution.py:605
  22.4 15.0 %collective-permute-start.6 = (f32[6,64,128]{2,1,0:T(8,128)S(1)}, f32[6,64,128]{2,1,0:T(8,128)S(1)}, u32[]{:S(2)}, u32[]{:S(2)}) collective-permute-start(f32[6,64,128]{2,1,0:T(8,128)S(1)} %get-tuple-element.40), channel_id=1, source_target_pairs={{0,16},{1,17},{2,18},{3,19},{4,20},{5,21},{6,22},{7,23},{8,24},{9,... | collective-permute-start | bytes 589832 | tf_op jit(solution)/shard_map/ppermute | solution.py:640
  29.5 22.1 %collective-permute-start.3 = (f32[8,64,128]{2,1,0:T(8,128)S(1)}, f32[8,64,128]{2,1,0:T(8,128)S(1)}, u32[]{:S(2)}, u32[]{:S(2)}) collective-permute-start(f32[8,64,128]{2,1,0:T(8,128)S(1)} %get-tuple-element.36), channel_id=1, source_target_pairs={{0,16},{1,17},{2,18},{3,19},{4,20},{5,21},{6,22},{7,23},{8,24},{9,... | collective-permute-start | bytes 786440 | tf_op jit(solution)/shard_map/ppermute | solution.py:640
  29.6 22.0 %collective-permute-start.7 = (f32[6,64,128]{2,1,0:T(8,128)S(1)}, f32[6,64,128]{2,1,0:T(8,128)S(1)}, u32[]{:S(2)}, u32[]{:S(2)}) collective-permute-start(f32[6,64,128]{2,1,0:T(8,128)S(1)} %get-tuple-element.41), channel_id=1, source_target_pairs={{0,1},{1,0},{2,3},{3,2},{4,5},{5,4},{6,7},{7,6},{8,9},{9,8},{10,11... | collective-permute-start | bytes 589832 | tf_op jit(solution)/shard_map/ppermute | solution.py:640
  31.5 20.1 %collective-permute-start.8 = (f32[6,64,128]{2,1,0:T(8,128)S(1)}, f32[6,64,128]{2,1,0:T(8,128)S(1)}, u32[]{:S(2)}, u32[]{:S(2)}) collective-permute-start(f32[6,64,128]{2,1,0:T(8,128)S(1)} %get-tuple-element.42), channel_id=1, source_target_pairs={{0,17},{1,16},{2,19},{3,18},{4,21},{5,20},{6,23},{7,22},{8,25},{9,... | collective-permute-start | bytes 589832 | tf_op jit(solution)/shard_map/ppermute | solution.py:640
  33.0 18.6 %collective-permute-start.4 = (f32[6,64,128]{2,1,0:T(8,128)S(1)}, f32[6,64,128]{2,1,0:T(8,128)S(1)}, u32[]{:S(2)}, u32[]{:S(2)}) collective-permute-start(f32[6,64,128]{2,1,0:T(8,128)S(1)} %get-tuple-element.37), channel_id=1, source_target_pairs={{0,1},{1,0},{2,3},{3,2},{4,5},{5,4},{6,7},{7,6},{8,9},{9,8},{10,11... | collective-permute-start | bytes 589832 | tf_op jit(solution)/shard_map/ppermute | solution.py:640
  37.4 14.2 %collective-permute-start.5 = (f32[6,64,128]{2,1,0:T(8,128)S(1)}, f32[6,64,128]{2,1,0:T(8,128)S(1)}, u32[]{:S(2)}, u32[]{:S(2)}) collective-permute-start(f32[6,64,128]{2,1,0:T(8,128)S(1)} %get-tuple-element.38), channel_id=1, source_target_pairs={{0,17},{1,16},{2,19},{3,18},{4,21},{5,20},{6,23},{7,22},{8,25},{9,... | collective-permute-start | bytes 589832 | tf_op jit(solution)/shard_map/ppermute | solution.py:640
